TPU v7x, 32 devices: a whole 2x2x4 slice. The times are simulated.
32 devices in a mesh: grp: 2 (over core), dp: 4 (over z), mp: 4 (over y, x).
Axes of the slice: x: 2, y: 2, z: 4, core: 2. Of those that a mesh axis runs over, the one named last changes fastest.
Arguments:
- hidden: bfloat16 [1024, 5120], P(('dp', 'mp')), may hold values from -6 to 6
- enc_weight: bfloat16 [5120, 8192], P(None, 'mp'), may hold values from -0.078125 to 0.078125
- enc_bias: bfloat16 [8192], P('mp'), may hold values from -5 to 5
- enc_frozen: bfloat16 [5120, 64], replicated, may hold values from -0.078125 to 0.078125
- enc_adapter: bfloat16 [64, 8192], P(None, 'mp'), may hold values from -0.75 to 0.75
- text_rows: bfloat16 [2560, 8192], P(('dp', 'mp')), may hold values from -6 to 6
- norm_gain: bfloat16 [8192], replicated, may hold values from 0.5 to 1.5
- value_weight: bfloat16 [8192, 1024], P(('dp', 'mp')), may hold values from -0.0625 to 0.0625
- value_bias: bfloat16 [1024], replicated, may hold values from -5 to 5
- llm_frozen: bfloat16 [8192, 64], P(('dp', 'mp')), may hold values from -0.0625 to 0.0625
- llm_adapter: bfloat16 [64, 1024], replicated, may hold values from -0.75 to 0.75
- targets: bfloat16 [2560, 1024], P(('dp', 'mp')), may hold values from -6 to 6
- dest_owner: int32 [1024, 1], replicated, may hold values from 0 to 15; in each aligned block of 256 rows (0 to 255, 256 to 511, ...) at most 32 rows name the same one
- seq_length: int32 [16], P(('dp', 'mp')), may hold values from 128 to 160
Outputs:
- grad_enc: float32 [64, 8192], P('grp', 'mp')
- grad_llm: float32 [64, 1024], P('grp')
Inputs may be any that keep to these rules, and one draw needn't show every extreme that they name: `dest_owner`: within the tokens of one encoder block (aligned blocks of 256 rows) no LLM device is named more than 32 times, and some device is named exactly 32 times in some blocks.
All inputs are finite; a program needn't handle non-finite values.
Results may differ from a plain program's by a relative error of at most 0.003.
Values may be sent and summed in bfloat16 or wider, within the bound.
A program may use at most 128 MiB of HBM per device.

v0:
```python
import jax
import jax.numpy as jnp
from jax import lax
from jax.sharding import PartitionSpec as P

ENC_DEV = 256
epsilon = 1e-06


def passed_along(value, axis, steps):
    count = lax.axis_size(axis)
    first, last = (max(0, -steps), min(count, count - steps))
    return lax.ppermute(value, axis, [(source, source + steps) for source in range(first, last)])


def swapped(array, axis, bit):
    return lax.ppermute(array, axis, [(i, i ^ 1 << bit) for i in range(lax.axis_size(axis))])


def slot_ranks(destiny, owners):
    markers = (destiny[:, None] == jnp.arange(owners, dtype=jnp.int32)[None, :]).astype(jnp.int32)
    return jnp.sum((jnp.cumsum(markers, axis=0) - markers) * markers, axis=1)


def body(
    hidden,
    enc_weight,
    enc_bias,
    enc_frozen,
    enc_adapter,
    text_rows,
    norm_gain,
    value_weight,
    value_bias,
    llm_frozen,
    llm_adapter,
    targets,
    dest_owner,
    seq_length,
):
    data_ways = lax.axis_size("dp")
    model_ways = lax.axis_size("mp")
    owners = data_ways * model_ways
    capacity = 2 * ENC_DEV // owners
    area = capacity * data_ways
    encoder = lax.axis_index("grp") == 0
    data_index = lax.axis_index("dp")
    owner_index = data_index * model_ways + lax.axis_index("mp")
    part_width = enc_weight.shape[1]
    rank_width = enc_frozen.shape[1]
    kv_width = llm_adapter.shape[1]
    group_rows = lax.all_gather(hidden, "mp", axis=0, tiled=True)

    def encode(source):
        low_rank = jnp.dot(source, enc_frozen, preferred_element_type=jnp.float32).astype(
            jnp.bfloat16
        )
        merged = jnp.dot(source, enc_weight, preferred_element_type=jnp.float32) + enc_bias.astype(
            jnp.float32
        )
        merged = merged + jnp.dot(low_rank, enc_adapter, preferred_element_type=jnp.float32)
        return (merged.astype(jnp.bfloat16), low_rank)

    def rest_encode(source):
        return (
            jnp.zeros((source.shape[0], part_width), jnp.bfloat16),
            jnp.zeros((source.shape[0], rank_width), jnp.bfloat16),
        )

    merged_rows, enc_low = lax.cond(encoder, encode, rest_encode, group_rows)
    destiny = dest_owner[:, 0]
    own_dest = lax.dynamic_slice_in_dim(destiny, data_index * ENC_DEV, ENC_DEV)
    bucket_index = slot_ranks(own_dest, owners) * owners + own_dest
    outgoing = (
        jnp.zeros((capacity * owners, part_width), jnp.bfloat16).at[bucket_index].set(merged_rows)
    )
    outgoing = outgoing.reshape(capacity, owners, part_width)
    grouped = lax.all_to_all(outgoing, ("dp", "mp"), split_axis=1, concat_axis=1, tiled=True)
    arrived = passed_along(grouped, "grp", 1)
    counts = jnp.sum((destiny.reshape(data_ways, ENC_DEV) == owner_index).astype(jnp.int32), axis=1)
    usable = (jnp.arange(capacity, dtype=jnp.int32)[:, None] < counts[None, :]).reshape(area, 1)
    gathered = (
        lax.all_gather(value_weight, ("dp", "mp"), axis=0, tiled=True),
        lax.all_gather(llm_frozen, ("dp", "mp"), axis=0, tiled=True),
    )

    def learn_layer(operands):
        incoming, whole_value, whole_frozen = operands
        image_rows = incoming.reshape(area, -1)
        head_rows = jnp.where(usable, image_rows, text_rows[:area])
        all_rows = jnp.concatenate([head_rows, text_rows[area:]], axis=0)
        wide_rows = all_rows.astype(jnp.float32)
        inverse = lax.rsqrt(jnp.mean(wide_rows * wide_rows, axis=1, keepdims=True) + epsilon)
        gain_wide = norm_gain.astype(jnp.float32)
        normed = (wide_rows * inverse * gain_wide).astype(jnp.bfloat16)
        low_rank = jnp.dot(normed, whole_frozen, preferred_element_type=jnp.float32).astype(
            jnp.bfloat16
        )
        values_out = jnp.dot(
            normed, whole_value, preferred_element_type=jnp.float32
        ) + value_bias.astype(jnp.float32)
        values_out = values_out + jnp.dot(low_rank, llm_adapter, preferred_element_type=jnp.float32)
        length = seq_length[0]
        position = jnp.arange(all_rows.shape[0], dtype=jnp.int32)
        row_weight = jnp.where(position < length, 1.0 / length.astype(jnp.float32), 0.0)
        dvalues = ((values_out - targets.astype(jnp.float32)) * row_weight[:, None]).astype(
            jnp.bfloat16
        )
        grad_part = jnp.dot(low_rank.T, dvalues, preferred_element_type=jnp.float32)
        head_dv = dvalues[:area]
        low_grad = jnp.dot(head_dv, llm_adapter.T, preferred_element_type=jnp.float32).astype(
            jnp.bfloat16
        )
        dnormed = jnp.dot(head_dv, whole_value.T, preferred_element_type=jnp.float32)
        dnormed = dnormed + jnp.dot(low_grad, whole_frozen.T, preferred_element_type=jnp.float32)
        scaled = gain_wide * dnormed
        head_wide = wide_rows[:area]
        head_inverse = inverse[:area]
        cubed = head_inverse * head_inverse * head_inverse
        image_grad = head_inverse * scaled - head_wide * cubed * jnp.mean(
            scaled * head_wide, axis=1, keepdims=True
        )
        image_grad = image_grad.astype(jnp.bfloat16)
        reply_rows = jnp.where(usable, image_grad, jnp.zeros_like(image_grad))
        return (grad_part, reply_rows.reshape(capacity, owners, part_width))

    def rest_learn(operands):
        return (
            jnp.zeros((rank_width, kv_width), jnp.float32),
            jnp.zeros((capacity, owners, part_width), jnp.bfloat16),
        )

    llm_part, reply_rows = lax.cond(
        encoder, rest_learn, learn_layer, (arrived, gathered[0], gathered[1])
    )
    llm_total = lax.psum(llm_part, ("dp", "mp"))
    grouped_back = lax.all_to_all(reply_rows, ("dp", "mp"), split_axis=1, concat_axis=1, tiled=True)
    returned = passed_along(grouped_back, "grp", -1)

    def adapt_grad(operands):
        back_rows, low_rank = operands
        image_grad = back_rows.reshape(capacity * owners, part_width)[bucket_index]
        return jnp.dot(low_rank.T, image_grad, preferred_element_type=jnp.float32)

    def rest_adapt(operands):
        return jnp.zeros((rank_width, part_width), jnp.float32)

    enc_part = lax.cond(encoder, adapt_grad, rest_adapt, (returned, enc_low))
    enc_total = lax.psum(enc_part, "dp")
    half_rank = rank_width // 2
    enc_count = half_rank * part_width
    llm_count = half_rank * kv_width
    span = max(enc_count, llm_count)
    enc_upper = enc_total[half_rank:].reshape(-1)
    llm_lower = jnp.pad(llm_total[:half_rank].reshape(-1), (0, span - llm_count))
    sending = jnp.where(encoder, enc_upper, llm_lower)
    received = swapped(sending, "grp", 0)
    grad_enc = jnp.where(encoder, enc_total[:half_rank], received.reshape(half_rank, part_width))
    grad_llm = jnp.where(
        encoder, received[:llm_count].reshape(half_rank, kv_width), llm_total[half_rank:]
    )
    return (grad_enc, grad_llm)


def solution(mesh):
    return jax.shard_map(
        body,
        mesh=mesh,
        in_specs=(
            P(("dp", "mp"), None),
            P(None, "mp"),
            P("mp"),
            P(),
            P(None, "mp"),
            P(("dp", "mp"), None),
            P(),
            P(("dp", "mp"), None),
            P(),
            P(("dp", "mp"), None),
            P(),
            P(("dp", "mp"), None),
            P(),
            P(("dp", "mp")),
        ),
        out_specs=(P("grp", "mp"), P("grp", None)),
        check_vma=False,
    )
```

profile of v0, /device:TPU:0, one launch (start us, length us, event | category | flops | bytes accessed | tf_op | source)
XLA Modules:
  0.0 564.6 jit_solution(298686897474769356)
XLA Ops:
  7.9 1.6 copy.49
  12.6 39.5 %all-gather.4.cloned.1.call-done = bf16[256,5120]{1,0:T(8,128)(2,1)} async-done(((bf16[64,5120]{1,0:T(8,128)(2,1)}), bf16[256,5120]{1,0:T(8,128)(2,1)}) %all-gather.4.cloned.1.call-update) | async-done | bytes 2621456 | tf_op jit(solution)/shard_map/all_gather | solution.py:52
  52.1 15.1 %conditional.3 = (bf16[256,2048]{1,0:T(8,128)(2,1)S(1)}, bf16[256,64]{0,1:T(8,128)(2,1)}) conditional(s32[]{:T(128)} %convert_element_type.60, () %tuple.31, (bf16[256,5120]{1,0:T(8,128)(2,1)}, bf16[5120,2048]{1,0:T(8,128)(2,1)}, bf16[2048]{0:T(1024)(128)(2,1)}, bf16[5120,64]{0,1:T(8,128)(2,1)}, bf16[64,2048]{1,0:T(8,128)(2,1)}) %tuple.32), branch_computations={%region_3.4_spmd, %region_4.5_spmd} | conditional | flops 5605181440 | bytes 44011620 | solution.py:70
  52.1 3.6 convolution_convert_fusion
  55.7 1.2 fusion.21
  56.9 10.3 %fusion.1 = bf16[256,2048]{1,0:T(8,128)(2,1)S(1)} fusion(f32[256,2048]{1,0:T(8,128)S(1)} %fusion.21, bf16[256,5120]{1,0:T(8,128)(2,1)S(1)} %copy-done.1, bf16[5120,2048]{1,0:T(8,128)(2,1)} %get-tuple-element.87, f32[2048]{0:T(1024)S(1)} %convert_element_type.42), kind=kOutput, calls=%fused_computation.4 | convolution fusion | flops 5370281984 | bytes 26746880 | tf_op jit(solution)/shard_map/cond/branch_1_fun/dot_general | solution.py:58
  68.2 3.5 scatter_custom_fusion
  71.7 1.2 copy.48
  72.9 59.7 %all_to_all.10 = bf16[32,16,2048]{2,0,1:T(8,128)(2,1)} all-to-all(bf16[32,16,2048]{2,0,1:T(8,128)(2,1)S(1)} %copy.48), channel_id=1, replica_groups=mesh['grp'=2,'dp'=4,'mp'=4] {'dp','mp'}, dimensions={1} | all-to-all | bytes 4194304 | tf_op jit(solution)/shard_map/all_to_all | solution.py:78
  132.6 1.4 collective-permute-start
  134.1 3.8 collective-permute-done
  137.9 183.1 %all-gather.8.cloned.1.call-done = bf16[8192,1024]{1,0:T(8,128)(2,1)} async-done(((bf16[512,1024]{1,0:T(8,128)(2,1)}), bf16[8192,1024]{1,0:T(8,128)(2,1)}) %all-gather.8.cloned.1.call-update) | async-done | bytes 16777232 | tf_op jit(solution)/shard_map/all_gather | solution.py:83
  321.6 1.2 copy.51
  322.8 31.6 %all_to_all.11 = bf16[32,16,2048]{2,0,1:T(8,128)(2,1)} all-to-all(bf16[32,16,2048]{2,0,1:T(8,128)(2,1)S(1)} %copy.51), channel_id=1, replica_groups=mesh['grp'=2,'dp'=4,'mp'=4] {'dp','mp'}, dimensions={1} | all-to-all | bytes 4194304 | tf_op jit(solution)/shard_map/all_to_all | solution.py:137
  354.3 1.3 collective-permute-start.1
  355.7 56.2 %collective-permute-done.1 = bf16[32,16,2048]{2,0,1:T(8,128)(2,1)S(1)} collective-permute-done((bf16[32,16,2048]{2,0,1:T(8,128)(2,1)}, bf16[32,16,2048]{2,0,1:T(8,128)(2,1)S(1)}, u32[]{:S(2)}, u32[]{:S(2)}) %collective-permute-start.1) | collective-permute-done | bytes 2097184 | tf_op jit(solution)/shard_map/ppermute | solution.py:13
  411.9 6.5 %conditional.5 = (f32[64,2048]{1,0:T(8,128)S(1)}) conditional(s32[]{:T(128)} %convert_element_type.60, () %tuple.30, (bf16[32,16,2048]{2,0,1:T(8,128)(2,1)S(1)}, s32[256]{0:T(256)S(1)}, s32[256]{0:T(256)S(1)}, bf16[256,64]{0,1:T(8,128)(2,1)}) %tuple.70), branch_computations={%region_11.12_spmd, %region_12.13_spmd} | conditional | flops 67111168 | bytes 16294948 | solution.py:148
  411.9 1.3 copy-done.3
  413.3 2.7 copy.52
  416.0 1.4 gather_fusion
  417.4 1.1 convolution_bitcast_fusion
  419.3 94.8 %all-reduce.6.cloned.1.call-done = f32[64,1024]{1,0:T(8,128)} async-done(((f32[64,1024]{1,0:T(8,128)}), f32[64,1024]{1,0:T(8,128)}) %all-reduce.6.cloned.1.call-update) | async-done | bytes 262160 | tf_op jit(solution)/shard_map/psum | solution.py:136
  515.1 38.7 %all-reduce.4.cloned.1.call-done = f32[64,2048]{1,0:T(8,128)} async-done(((f32[64,2048]{1,0:T(8,128)}), f32[64,2048]{1,0:T(8,128)}) %all-reduce.4.cloned.1.call-update) | async-done | bytes 524304 | tf_op jit(solution)/shard_map/psum | solution.py:149
  555.0 1.5 collective-permute-done.2
  (65 shorter events, 10.2 us)
Async XLA Ops:
  7.2 44.9 %all-gather.4.cloned.1.call-start = ((), (), s32[]{:S(2)}) async-start(), calls=%async_computation.2 | async-start | bytes 3276800 | tf_op jit(solution)/shard_map/all_gather | solution.py:52
  7.9 126.2 %all-gather.6.cloned.1.call-start = ((), (), s32[]{:S(2)}) async-start(), calls=%async_computation.3 | async-start | bytes 2228224 | tf_op jit(solution)/shard_map/all_gather | solution.py:84
  9.6 311.5 %all-gather.8.cloned.1.call-start = ((), (), s32[]{:S(2)}) async-start(), calls=%async_computation.4 | async-start | bytes 17825792 | tf_op jit(solution)/shard_map/all_gather | solution.py:83
  10.3 503.8 %all-reduce.6.cloned.1.call-start = ((), (), s32[]{:S(2)}) async-start(), calls=%async_computation.6 | async-start | bytes 524288 | tf_op jit(solution)/shard_map/psum | solution.py:136
  52.1 3.6 copy-start.11
  52.1 4.8 copy-start.15
  52.1 4.8 copy-start.1
  67.2 1.0 copy-start.6
  72.9 248.2 %copy-start.8 = (bf16[64,1024]{1,0:T(8,128)(2,1)S(1)}, bf16[64,1024]{1,0:T(8,128)(2,1)}, u32[]{:S(2)}) copy-start(bf16[64,1024]{1,0:T(8,128)(2,1)} %param.30) | copy-start | bytes 393220
  72.9 248.2 %copy-start.10 = (bf16[160,1024]{1,0:T(8,128)(2,1)S(1)}, bf16[160,1024]{1,0:T(8,128)(2,1)}, u32[]{:S(2)}) copy-start(bf16[160,1024]{1,0:T(8,128)(2,1)} %param.31) | copy-start | bytes 983044
  72.9 248.2 %copy-start.13 = (bf16[8192]{0:T(1024)(128)(2,1)S(1)}, bf16[8192]{0:T(1024)(128)(2,1)}, u32[]{:S(2)}) copy-start(bf16[8192]{0:T(1024)(128)(2,1)} %param.26) | copy-start | bytes 49156
  72.9 248.2 %copy-start.14 = (s32[1024,1]{0,1:T(1,128)S(1)}, s32[1024,1]{0,1:T(1,128)}, u32[]{:S(2)}) copy-start(s32[1024,1]{0,1:T(1,128)} %param.32) | copy-start | bytes 12292
  72.9 248.2 %copy-start.16 = (bf16[1024]{0:T(1024)(128)(2,1)S(1)}, bf16[1024]{0:T(1024)(128)(2,1)}, u32[]{:S(2)}) copy-start(bf16[1024]{0:T(1024)(128)(2,1)} %param.28) | copy-start | bytes 6148
  132.6 5.3 collective-permute-start
  321.6 32.8 %copy-start.7 = (f32[64,1024]{1,0:T(8,128)}, f32[64,1024]{1,0:T(8,128)S(1)}, u32[]{:S(2)}) copy-start(f32[64,1024]{1,0:T(8,128)S(1)} %get-tuple-element.82) | copy-start | bytes 786436
  354.3 57.6 %collective-permute-start.1 = (bf16[32,16,2048]{2,0,1:T(8,128)(2,1)}, bf16[32,16,2048]{2,0,1:T(8,128)(2,1)S(1)}, u32[]{:S(2)}, u32[]{:S(2)}) collective-permute-start(bf16[32,16,2048]{2,0,1:T(8,128)(2,1)} %all_to_all.11), channel_id=1, source_target_pairs={{16,0},{17,1},{18,2},{19,3},{20,4},{21,5},{22,6},{23,7},{24,8},{25... | collective-permute-start | bytes 6291464 | tf_op jit(solution)/shard_map/ppermute | solution.py:13
  355.7 198.1 %all-reduce.4.cloned.1.call-start = ((), (), s32[]{:S(2)}) async-start(), calls=%async_computation.5 | async-start | bytes 1048576 | tf_op jit(solution)/shard_map/psum | solution.py:149
  411.9 1.3 copy-start.3
  418.5 0.8 copy-start.4
  514.1 43.3 %copy-start.12 = (f32[64,1024]{1,0:T(8,128)S(1)}, f32[64,1024]{1,0:T(8,128)}, u32[]{:S(2)}) copy-start(f32[64,1024]{1,0:T(8,128)} %all-reduce.6.cloned.1.call-done) | copy-start | bytes 786436
  553.8 2.8 copy-start.9
  554.9 1.6 collective-permute-start.2
Sparse Core Ops, SparseCore 0:
  9.8 42.2 all-gather.3
  55.5 72.8 all-gather.5
  131.1 189.8 all-gather.7
  355.8 158.2 all-reduce.5
  516.3 37.5 all-reduce.3
where the time goes:
time: 565 us
  waiting for transfers between devices  419 us (74%)
  blocking collectives  91.3 us (16%)
  local copies, waits for them, and re-layouts  18 us (3%)
  matrix products  16.1 us (3%)
  between operations  14 us (2%)
    all_gather x1, waiting for transfers between devices, body(): lax.all_gather(value_weight, ('dp', 'mp'), axis=0, tiled=True)  183 us
    psum x1, waiting for transfers between devices, body(): llm_total = lax.psum(llm_part, ('dp', 'mp'))  94.8 us
    ppermute x2, waiting for transfers between devices, passed_along(): lax.ppermute(value, axis, [(source, source + steps) for source in range(f...  60 us
    all_to_all x1, blocking collectives, body(): lax.all_to_all(outgoing, ('dp', 'mp'), split_axis=1, concat_axis=1, tiled...  59.7 us
    all_gather x1, waiting for transfers between devices, body(): group_rows = lax.all_gather(hidden, 'mp', axis=0, tiled=True)  39.5 us
    psum x1, waiting for transfers between devices, body(): enc_total = lax.psum(enc_part, 'dp')  38.7 us
    all_to_all x1, blocking collectives, body(): lax.all_to_all(reply_rows, ('dp', 'mp'), split_axis=1, concat_axis=1, til...  31.6 us
  transfers between devices with their start and end apart: 8, of which 7 were waited for; matrix products, arithmetic and copies ran while one was open for 5% of the time, Pallas kernels for 0%

commit v1 on v0

--- a/solution.py
+++ b/solution.py
@@ -49,7 +49,12 @@
     part_width = enc_weight.shape[1]
     rank_width = enc_frozen.shape[1]
     kv_width = llm_adapter.shape[1]
-    group_rows = lax.all_gather(hidden, "mp", axis=0, tiled=True)
+    ring = [hidden]
+    for hop in range(3):
+        ring.append(lax.ppermute(ring[-1], "mp", [(dev, (dev + 1) % 4) for dev in range(4)]))
+    group_rows = jnp.roll(
+        jnp.concatenate(ring[::-1], axis=0), (lax.axis_index("mp") + 1) * ring[0].shape[0], axis=0
+    )
 
     def encode(source):
         low_rank = jnp.dot(source, enc_frozen, preferred_element_type=jnp.float32).astype(

time: 565 us -> 542 us (0.959)
  waiting for transfers between devices: 419 us -> 388 us
    ppermute x0 -> x3, waiting for transfers between devices: none -> 50.8 us  [body(): lax.ppermute(ring[-1], 'mp', [(dev, (dev + 1) % 4) for dev in range(4)])]
    all_gather x1, waiting for transfers between devices: 183 us -> 141 us  [body(): lax.all_gather(value_weight, ('dp', 'mp'), axis=0, tiled=True)]
    all_gather x1 -> x0, waiting for transfers between devices: 39.5 us -> none  [body(): group_rows = lax.all_gather(hidden, 'mp', axis=0, tiled=True)]
  transfers between devices with their start and end apart: 8 -> 10, of which waited for: 7 -> 9; matrix products, arithmetic and copies ran while one was open for 5% -> 6% of each run, Pallas kernels for 0% -> 0%
where the time goes in v1:
time: 542 us
  waiting for transfers between devices  388 us (72%)
  blocking collectives  88.8 us (16%)
  local copies, waits for them, and re-layouts  23.3 us (4%)
  matrix products  16.3 us (3%)
  between operations  14 us (3%)
  starting transfers between devices  6.73 us (1%)
    all_gather x1, waiting for transfers between devices, body(): lax.all_gather(value_weight, ('dp', 'mp'), axis=0, tiled=True)  141 us
    psum x1, waiting for transfers between devices, body(): llm_total = lax.psum(llm_part, ('dp', 'mp'))  94.7 us
    ppermute x2, waiting for transfers between devices, passed_along(): lax.ppermute(value, axis, [(source, source + steps) for source in range(f...  60 us
    all_to_all x1, blocking collectives, body(): lax.all_to_all(outgoing, ('dp', 'mp'), split_axis=1, concat_axis=1, tiled...  57.2 us
    ppermute x3, waiting for transfers between devices, body(): lax.ppermute(ring[-1], 'mp', [(dev, (dev + 1) % 4) for dev in range(4)])  50.8 us
    psum x1, waiting for transfers between devices, body(): enc_total = lax.psum(enc_part, 'dp')  38.8 us
    all_to_all x1, blocking collectives, body(): lax.all_to_all(reply_rows, ('dp', 'mp'), split_axis=1, concat_axis=1, til...  31.6 us
  transfers between devices with their start and end apart: 10, of which 9 were waited for; matrix products, arithmetic and copies ran while one was open for 6% of the time, Pallas kernels for 0%

profile of v1, /device:TPU:0, one launch (start us, length us, event | category | flops | bytes accessed | tf_op | source)
XLA Modules:
  0.0 541.7 jit_solution(866493241003923914)
XLA Ops:
  7.2 1.7 copy.53
  9.7 3.0 collective-permute-start
  12.7 16.8 %collective-permute-done = bf16[64,5120]{1,0:T(8,128)(2,1)S(1)} collective-permute-done((bf16[64,5120]{1,0:T(8,128)(2,1)}, bf16[64,5120]{1,0:T(8,128)(2,1)S(1)}, u32[]{:S(2)}, u32[]{:S(2)}) %collective-permute-start) | collective-permute-done | bytes 655392 | tf_op jit(solution)/shard_map/ppermute | solution.py:54
  31.6 18.4 %collective-permute-done.1 = bf16[64,5120]{1,0:T(8,128)(2,1)S(1)} collective-permute-done((bf16[64,5120]{1,0:T(8,128)(2,1)S(1)}, bf16[64,5120]{1,0:T(8,128)(2,1)S(1)}, u32[]{:S(2)}, u32[]{:S(2)}) %collective-permute-start.1) | collective-permute-done | bytes 655392 | tf_op jit(solution)/shard_map/ppermute | solution.py:54
  51.1 15.5 %collective-permute-done.2 = bf16[64,5120]{1,0:T(8,128)(2,1)S(1)} collective-permute-done((bf16[64,5120]{1,0:T(8,128)(2,1)S(1)}, bf16[64,5120]{1,0:T(8,128)(2,1)S(1)}, u32[]{:S(2)}, u32[]{:S(2)}) %collective-permute-start.2) | collective-permute-done | bytes 655392 | tf_op jit(solution)/shard_map/ppermute | solution.py:54
  73.7 15.3 %conditional.3 = (bf16[256,2048]{1,0:T(8,128)(2,1)S(1)}, bf16[256,64]{0,1:T(8,128)(2,1)}) conditional(s32[]{:T(128)} %convert_element_type.69, () %tuple.39, (s32[]{:T(128)}, s32[]{:T(128)}, bf16[512,5120]{1,0:T(8,128)(2,1)}, bf16[5120,2048]{1,0:T(8,128)(2,1)}, bf16[2048]{0:T(1024)(128)(2,1)S(1)}, /*index=5*/bf16[5120,64]{0,1:T(8,128)(2,1)}, ...), branch_computations={%region_3.4_spmd, %region_4.5_spmd.clone} | conditional | flops 5605181440 | bytes 32460980 | solution.py:75
  73.7 3.4 fusion.5
  78.3 10.7 %fusion.1 = bf16[256,2048]{1,0:T(8,128)(2,1)S(1)} fusion(f32[256,2048]{1,0:T(8,128)S(1)} %fusion.29, bf16[5120,2048]{1,0:T(8,128)(2,1)} %get-tuple-element.217, bf16[512,5120]{1,0:T(8,128)(2,1)} %get-tuple-element.213, s32[]{:T(128)S(6)} %select_n.78, f32[2048]{0:T(1024)S(1)} %convert_element_type.76), kind=kOutput, calls=%fused_computation.4 | convolution fusion | flops 5370281984 | bytes 26746884 | tf_op jit(solution)/shard_map/cond/branch_1_fun/dot_general | solution.py:63
  89.0 2.8 scatter_custom_fusion
  93.1 57.2 %all_to_all.10 = bf16[32,16,2048]{2,0,1:T(8,128)(2,1)} all-to-all(bf16[32,16,2048]{2,0,1:T(8,128)(2,1)S(1)} %copy.52), channel_id=1, replica_groups=mesh['grp'=2,'dp'=4,'mp'=4] {'dp','mp'}, dimensions={1} | all-to-all | bytes 4194304 | tf_op jit(solution)/shard_map/all_to_all | solution.py:83
  150.3 1.4 collective-permute-start.3
  151.7 3.8 collective-permute-done.3
  155.5 141.0 %all-gather.5.cloned.1.call-done = bf16[8192,1024]{1,0:T(8,128)(2,1)} async-done(((bf16[512,1024]{1,0:T(8,128)(2,1)}), bf16[8192,1024]{1,0:T(8,128)(2,1)}) %all-gather.5.cloned.1.call-update) | async-done | bytes 16777232 | tf_op jit(solution)/shard_map/all_gather | solution.py:88
  298.2 31.6 %all_to_all.11 = bf16[32,16,2048]{2,0,1:T(8,128)(2,1)} all-to-all(bf16[32,16,2048]{2,0,1:T(8,128)(2,1)S(1)} %copy.55), channel_id=1, replica_groups=mesh['grp'=2,'dp'=4,'mp'=4] {'dp','mp'}, dimensions={1} | all-to-all | bytes 4194304 | tf_op jit(solution)/shard_map/all_to_all | solution.py:142
  331.2 56.2 %collective-permute-done.4 = bf16[32,16,2048]{2,0,1:T(8,128)(2,1)S(1)} collective-permute-done((bf16[32,16,2048]{2,0,1:T(8,128)(2,1)}, bf16[32,16,2048]{2,0,1:T(8,128)(2,1)S(1)}, u32[]{:S(2)}, u32[]{:S(2)}) %collective-permute-start.4) | collective-permute-done | bytes 2097184 | tf_op jit(solution)/shard_map/ppermute | solution.py:13
  387.4 6.5 %conditional.5 = (f32[64,2048]{1,0:T(8,128)S(1)}) conditional(s32[]{:T(128)} %convert_element_type.69, () %tuple.38, (bf16[32,16,2048]{2,0,1:T(8,128)(2,1)S(1)}, s32[256]{0:T(256)S(1)}, s32[256]{0:T(256)S(1)}, bf16[256,64]{0,1:T(8,128)(2,1)}) %tuple.85), branch_computations={%region_11.12_spmd, %region_12.13_spmd} | conditional | flops 67111168 | bytes 16294948 | solution.py:153
  387.4 1.3 copy-done.3
  388.7 2.7 copy.56
  391.5 1.4 gather_fusion
  394.7 94.7 %all-reduce.6.cloned.1.call-done = f32[64,1024]{1,0:T(8,128)} async-done(((f32[64,1024]{1,0:T(8,128)}), f32[64,1024]{1,0:T(8,128)}) %all-reduce.6.cloned.1.call-update) | async-done | bytes 262160 | tf_op jit(solution)/shard_map/psum | solution.py:141
  490.4 38.8 %all-reduce.4.cloned.1.call-done = f32[64,2048]{1,0:T(8,128)} async-done(((f32[64,2048]{1,0:T(8,128)}), f32[64,2048]{1,0:T(8,128)}) %all-reduce.4.cloned.1.call-update) | async-done | bytes 524304 | tf_op jit(solution)/shard_map/psum | solution.py:154
  530.3 1.5 collective-permute-done.5
  532.0 1.7 slice_select_fusion.1
  533.6 1.6 slice_select_fusion.2
  (70 shorter events, 20.7 us)
Async XLA Ops:
  7.2 62.1 %copy-start.1 = (bf16[64,5120]{1,0:T(8,128)(2,1)S(1)}, bf16[64,5120]{1,0:T(8,128)(2,1)}, u32[]{:S(2)}) copy-start(bf16[64,5120]{1,0:T(8,128)(2,1)} %param.20) | copy-start | bytes 1966084
  7.2 144.5 %all-gather.3.cloned.1.call-start = ((), (), s32[]{:S(2)}) async-start(), calls=%async_computation.2 | async-start | bytes 2228224 | tf_op jit(solution)/shard_map/all_gather | solution.py:89
  8.9 287.6 %all-gather.5.cloned.1.call-start = ((), (), s32[]{:S(2)}) async-start(), calls=%async_computation.3 | async-start | bytes 17825792 | tf_op jit(solution)/shard_map/all_gather | solution.py:88
  9.7 479.8 %all-reduce.6.cloned.1.call-start = ((), (), s32[]{:S(2)}) async-start(), calls=%async_computation.5 | async-start | bytes 524288 | tf_op jit(solution)/shard_map/psum | solution.py:141
  9.7 19.9 %collective-permute-start = (bf16[64,5120]{1,0:T(8,128)(2,1)}, bf16[64,5120]{1,0:T(8,128)(2,1)S(1)}, u32[]{:S(2)}, u32[]{:S(2)}) collective-permute-start(bf16[64,5120]{1,0:T(8,128)(2,1)} %param.20), channel_id=1, source_target_pairs={{0,1},{1,2},{2,3},{3,0},{4,5},{5,6},{6,7},{7,4},{8,9},{9,10},{10,1... | collective-permute-start | bytes 1966088 | tf_op jit(solution)/shard_map/ppermute | solution.py:54
  29.6 20.5 %collective-permute-start.1 = (bf16[64,5120]{1,0:T(8,128)(2,1)S(1)}, bf16[64,5120]{1,0:T(8,128)(2,1)S(1)}, u32[]{:S(2)}, u32[]{:S(2)}) collective-permute-start(bf16[64,5120]{1,0:T(8,128)(2,1)S(1)} %collective-permute-done), channel_id=1, source_target_pairs={{0,1},{1,2},{2,3},{3,0},{4,5},{5,6},{6,7},{7,4},{8,9},{9,10},{10,1... | collective-permute-start | bytes 1966088 | tf_op jit(solution)/shard_map/ppermute | solution.py:54
  50.0 16.5 %collective-permute-start.2 = (bf16[64,5120]{1,0:T(8,128)(2,1)S(1)}, bf16[64,5120]{1,0:T(8,128)(2,1)S(1)}, u32[]{:S(2)}, u32[]{:S(2)}) collective-permute-start(bf16[64,5120]{1,0:T(8,128)(2,1)S(1)} %collective-permute-done.1), channel_id=1, source_target_pairs={{0,1},{1,2},{2,3},{3,0},{4,5},{5,6},{6,7},{7,4},{8,9},{9,10},{10,1... | collective-permute-start | bytes 1966088 | tf_op jit(solution)/shard_map/ppermute | solution.py:54
  68.3 5.4 copy-start.9
  68.3 5.4 copy-start.12
  91.8 204.7 %copy-start.7 = (bf16[64,1024]{1,0:T(8,128)(2,1)S(1)}, bf16[64,1024]{1,0:T(8,128)(2,1)}, u32[]{:S(2)}) copy-start(bf16[64,1024]{1,0:T(8,128)(2,1)} %param.30) | copy-start | bytes 393220
  91.8 204.7 %copy-start.8 = (bf16[160,1024]{1,0:T(8,128)(2,1)S(1)}, bf16[160,1024]{1,0:T(8,128)(2,1)}, u32[]{:S(2)}) copy-start(bf16[160,1024]{1,0:T(8,128)(2,1)} %param.31) | copy-start | bytes 983044
  91.9 204.7 %copy-start.10 = (bf16[8192]{0:T(1024)(128)(2,1)S(1)}, bf16[8192]{0:T(1024)(128)(2,1)}, u32[]{:S(2)}) copy-start(bf16[8192]{0:T(1024)(128)(2,1)} %param.26) | copy-start | bytes 49156
  91.9 204.7 %copy-start.11 = (s32[1024,1]{0,1:T(1,128)S(1)}, s32[1024,1]{0,1:T(1,128)}, u32[]{:S(2)}) copy-start(s32[1024,1]{0,1:T(1,128)} %param.32) | copy-start | bytes 12292
  91.9 204.7 %copy-start.13 = (bf16[1024]{0:T(1024)(128)(2,1)S(1)}, bf16[1024]{0:T(1024)(128)(2,1)}, u32[]{:S(2)}) copy-start(bf16[1024]{0:T(1024)(128)(2,1)} %param.28) | copy-start | bytes 6148
  150.3 5.3 collective-permute-start.3
  297.1 32.8 %copy-start.6 = (f32[64,1024]{1,0:T(8,128)}, f32[64,1024]{1,0:T(8,128)S(1)}, u32[]{:S(2)}) copy-start(f32[64,1024]{1,0:T(8,128)S(1)} %get-tuple-element.177) | copy-start | bytes 786436
  329.8 57.5 %collective-permute-start.4 = (bf16[32,16,2048]{2,0,1:T(8,128)(2,1)}, bf16[32,16,2048]{2,0,1:T(8,128)(2,1)S(1)}, u32[]{:S(2)}, u32[]{:S(2)}) collective-permute-start(bf16[32,16,2048]{2,0,1:T(8,128)(2,1)} %all_to_all.11), channel_id=1, source_target_pairs={{16,0},{17,1},{18,2},{19,3},{20,4},{21,5},{22,6},{23,7},{24,8},{25... | collective-permute-start | bytes 6291464 | tf_op jit(solution)/shard_map/ppermute | solution.py:13
  331.1 198.0 %all-reduce.4.cloned.1.call-start = ((), (), s32[]{:S(2)}) async-start(), calls=%async_computation.4 | async-start | bytes 1048576 | tf_op jit(solution)/shard_map/psum | solution.py:154
  387.4 1.3 copy-start.3
  393.9 0.8 copy-start.4
  530.2 1.6 collective-permute-start.5
Sparse Core Ops, SparseCore 0:
  11.3 68.5 all-gather.2
  82.7 213.7 all-gather.4
  331.3 158.1 all-reduce.5
  491.6 37.5 all-reduce.3
